TPU v7x, 32 devices: a whole 2x2x4 slice. The times are simulated.
32 devices in a mesh: node: 8 (over y, x, core), grp: 4 (over z).
Axes of the slice: x: 2, y: 2, z: 4, core: 2. Of those that a mesh axis runs over, the one named last changes fastest.
Arguments:
- tokens: bfloat16 [12288, 1792], P(('node', 'grp')), may hold values from -6 to 6
- cotangent: bfloat16 [12288, 1792], P(('node', 'grp')), may hold values from -6 to 6
- gate_weight: bfloat16 [1792, 1024], P('node'), may hold values from -0.125 to 0.125
- up_weight: bfloat16 [1792, 1024], P('node'), may hold values from -0.125 to 0.125
- down_weight_t: bfloat16 [1792, 1024], P('node'), may hold values from -0.125 to 0.125
- error_memory: bfloat16 [4, 1792, 3072], P('grp', 'node'), may hold values from -4 to 4
- q_init: float32 [3, 1024, 32], replicated, may hold values from -6 to 6
Outputs:
- token_grad: bfloat16 [12288, 1792], P(('node', 'grp'))
- new_error: bfloat16 [4, 1792, 3072], P('grp', 'node')
- p_hat: float32 [3, 1792, 32], P(None, 'node')
- q_new: float32 [3, 1024, 32], replicated
All inputs are finite; a program needn't handle non-finite values.
Results may differ from a plain program's by a relative error of at most 0.012.
Values may be sent and summed in bfloat16 or wider, within the bound.
A program may use at most 192 MiB of HBM per device.

v0:
```python
import math

import jax
import jax.numpy as jnp
from jax import lax
from jax.sharding import PartitionSpec as P


def gelu_parts(value):
    coeff = math.sqrt(2.0 / math.pi)
    inner = coeff * (value + 0.044715 * value * value * value)
    tanh_value = jnp.tanh(inner)
    activation = 0.5 * value * (1.0 + tanh_value)
    slope = 0.5 * (1.0 + tanh_value) + 0.5 * value * (1.0 - tanh_value * tanh_value) * coeff * (
        1.0 + 3.0 * 0.044715 * value * value
    )
    return (activation, slope)


def contract_rows(left_side, right_side):
    return lax.dot_general(
        left_side, right_side, (((0,), (0,)), ((), ())), preferred_element_type=jnp.float32
    )


def on_device(tokens, cotangent, gate_weight, up_weight, down_weight_t, error_memory, q_init):
    node_count = lax.axis_size("node")
    group_count = lax.axis_size("grp")
    hidden_units = gate_weight.shape[1]
    highest = lax.Precision.HIGHEST
    full_gate, full_up, full_down = (
        lax.all_gather(gate_weight, "node", axis=0, tiled=True),
        lax.all_gather(up_weight, "node", axis=0, tiled=True),
        lax.all_gather(down_weight_t, "node", axis=0, tiled=True),
    )
    gate_pre = jnp.dot(tokens, full_gate, preferred_element_type=jnp.float32)
    up_pre = jnp.dot(tokens, full_up, preferred_element_type=jnp.float32)
    activation, slope = gelu_parts(gate_pre)
    hidden = (activation * up_pre).astype(jnp.bfloat16)
    back_hidden = jnp.dot(cotangent, full_down, preferred_element_type=jnp.float32)
    grad_up = (back_hidden * activation).astype(jnp.bfloat16)
    grad_gate = (back_hidden * up_pre * slope).astype(jnp.bfloat16)
    token_grad = (
        lax.dot_general(
            grad_gate, full_gate, (((1,), (1,)), ((), ())), preferred_element_type=jnp.float32
        )
        + lax.dot_general(
            grad_up, full_up, (((1,), (1,)), ((), ())), preferred_element_type=jnp.float32
        )
    ).astype(jnp.bfloat16)
    gate_up = jnp.concatenate([grad_gate, grad_up], axis=1)
    token_cols, cot_cols = (
        lax.all_to_all(tokens, "node", split_axis=1, concat_axis=0, tiled=True),
        lax.all_to_all(cotangent, "node", split_axis=1, concat_axis=0, tiled=True),
    )
    piece_gu = lax.all_gather(gate_up, "node", axis=0, tiled=True)
    piece_hidden = lax.all_gather(hidden, "node", axis=0, tiled=True)
    summed = jnp.concatenate(
        [contract_rows(token_cols, piece_gu), contract_rows(cot_cols, piece_hidden)], axis=1
    )
    grad_scale = 1.0 / math.sqrt(tokens.shape[0] * node_count)
    merged = summed * grad_scale + error_memory[0].astype(jnp.float32)
    blocks = [merged[:, m * hidden_units : (m + 1) * hidden_units] for m in range(3)]
    row_terms = jnp.stack([jnp.dot(blocks[m], q_init[m], precision=highest) for m in range(3)])
    power_rows = lax.psum(row_terms.astype(jnp.bfloat16), "grp").astype(jnp.float32) / group_count
    local_gram = jnp.einsum("mdr,mds->mrs", power_rows, power_rows, precision=highest)
    gram_matrix = lax.psum(local_gram, "node")
    hats = []
    for m in range(3):
        factor = jnp.linalg.cholesky(gram_matrix[m])
        hats.append(jax.scipy.linalg.solve_triangular(factor, power_rows[m].T, lower=True).T)
    col_terms = jnp.stack([jnp.dot(blocks[m].T, hats[m], precision=highest) for m in range(3)])
    q_new = lax.psum(col_terms, ("node", "grp")) / group_count
    errors = [blocks[m] - jnp.dot(hats[m], q_new[m].T, precision=highest) for m in range(3)]
    new_error = jnp.concatenate(errors, axis=1).astype(jnp.bfloat16)[None]
    return (token_grad, new_error, jnp.stack(hats), q_new)


def solution(mesh):
    return jax.shard_map(
        on_device,
        mesh=mesh,
        in_specs=(
            P(("node", "grp"), None),
            P(("node", "grp"), None),
            P("node", None),
            P("node", None),
            P("node", None),
            P("grp", "node", None),
            P(),
        ),
        out_specs=(P(("node", "grp"), None), P("grp", "node", None), P(None, "node", None), P()),
        check_vma=False,
    )
```

profile of v0, /device:TPU:0, one launch (start us, length us, event | category | flops | bytes accessed | tf_op | source)
XLA Modules:
  0.0 512.1 jit_solution(15546751805123783097)
XLA Ops:
  9.4 37.6 %all-gather.6.cloned.1.call-done = bf16[1792,1024]{1,0:T(8,128)(2,1)} async-done(((bf16[224,1024]{1,0:T(8,128)(2,1)}), bf16[1792,1024]{1,0:T(8,128)(2,1)}) %all-gather.6.cloned.1.call-update) | async-done | bytes 3670032 | tf_op jit(solution)/shard_map/all_gather | solution.py:34
  47.0 5.2 %fusion.44 = f32[384,1024]{1,0:T(8,128)} fusion(bf16[384,1792]{1,0:T(8,128)(2,1)} %param.11, bf16[1792,1024]{1,0:T(8,128)(2,1)} %all-gather.6.cloned.1.call-done), kind=kOutput, calls=%fused_computation.92 | convolution fusion | flops 1409286144 | bytes 6619136 | tf_op jit(solution)/shard_map/dot_general | solution.py:40
  52.2 31.1 %all-gather.10.cloned.1.call-done = bf16[1792,1024]{1,0:T(8,128)(2,1)} async-done(((bf16[224,1024]{1,0:T(8,128)(2,1)}), bf16[1792,1024]{1,0:T(8,128)(2,1)}) %all-gather.10.cloned.1.call-update) | async-done | bytes 3670032 | tf_op jit(solution)/shard_map/all_gather | solution.py:32
  83.3 4.8 fusion.45
  88.1 31.5 %all-gather.8.cloned.1.call-done = bf16[1792,1024]{1,0:T(8,128)(2,1)} async-done(((bf16[224,1024]{1,0:T(8,128)(2,1)}), bf16[1792,1024]{1,0:T(8,128)(2,1)}) %all-gather.8.cloned.1.call-update) | async-done | bytes 3670032 | tf_op jit(solution)/shard_map/all_gather | solution.py:33
  119.6 6.4 %multiply_convert_fusion = (bf16[384,1024]{1,0:T(8,128)(2,1)}, bf16[384,1024]{1,0:T(8,128)(2,1)S(1)}, bf16[384,1024]{1,0:T(8,128)(2,1)S(1)}) fusion(f32[384,1024]{1,0:T(8,128)} %fusion.45, f32[384,1024]{1,0:T(8,128)} %fusion.44, bf16[384,1792]{1,0:T(8,128)(2,1)S(1)} %copy-done.2, bf16[1792,1024]{1,0:T(8,128)(2,1)} %all-gather.8.cloned.1.call-done), kind=kOutput, calls=%fused_computation.15 | convolution fusion | flops 1419116544 | bytes 10551296 | tf_op jit(solution)/shard_map/dot_general | solution.py:37
  131.1 3.6 all-to-all-start.1
  136.3 24.3 %all-to-all-done.1 = bf16[384,8,224]{0,2,1:T(8,128)(2,1)S(1)} async-done(((bf16[384,8,224]{0,2,1:T(8,128)(2,1)}), bf16[384,8,224]{0,2,1:T(8,128)(2,1)S(1)}, u32[]{:S(2)}, u32[]{:S(2)}) %all-to-all-start.1) | async-done | bytes 1376288 | tf_op jit(solution)/shard_map/all_to_all | solution.py:54
  160.5 3.6 all-to-all-start
  165.7 31.9 %all-to-all-done = bf16[384,8,224]{0,2,1:T(8,128)(2,1)S(1)} async-done(((bf16[384,8,224]{0,2,1:T(8,128)(2,1)}), bf16[384,8,224]{0,2,1:T(8,128)(2,1)S(1)}, u32[]{:S(2)}, u32[]{:S(2)}) %all-to-all-start) | async-done | bytes 1376288 | tf_op jit(solution)/shard_map/all_to_all | solution.py:53
  198.9 5.4 %fusion.46 = f32[384,1792]{1,0:T(8,128)} fusion(bf16[384,1024]{1,0:T(8,128)(2,1)S(1)} %copy-done.8, bf16[1792,1024]{1,0:T(8,128)(2,1)} %all-gather.10.cloned.1.call-done), kind=kOutput, calls=%fused_computation.94 | convolution fusion | flops 1409286144 | bytes 7208960 | tf_op jit(solution)/shard_map/dot_general | solution.py:44
  204.3 5.4 %convolution_bitcast_fusion.1 = f32[224,1024]{1,0:T(8,128)} fusion(bf16[3072,224]{0,1:T(8,128)(2,1)S(1)} %bitcast.133, bf16[3072,1024]{1,0:T(8,128)(2,1)} %all-gather.14.cloned.1.call-done), kind=kOutput, calls=%fused_computation.19 | convolution fusion | flops 1409286144 | bytes 8585216 | tf_op jit(solution)/shard_map/dot_general | solution.py:21
  209.7 64.7 %all-gather.12.cloned.1.call-done = bf16[3072,2048]{1,0:T(8,128)(2,1)} async-done(((bf16[384,2048]{1,0:T(8,128)(2,1)}), bf16[3072,2048]{1,0:T(8,128)(2,1)}) %all-gather.12.cloned.1.call-update) | async-done | bytes 12582928 | tf_op jit(solution)/shard_map/all_gather | solution.py:56
  274.4 6.4 %convolution_bitcast_fusion = f32[224,2048]{1,0:T(8,128)S(1)} fusion(bf16[3072,224]{0,1:T(8,128)(2,1)S(1)} %bitcast.134, bf16[3072,2048]{1,0:T(8,128)(2,1)} %all-gather.12.cloned.1.call-done), kind=kOutput, calls=%fused_computation.4 | convolution fusion | flops 2818572288 | bytes 15794176 | tf_op jit(solution)/shard_map/dot_general | solution.py:21
  285.2 20.5 %psum.21 = bf16[3,224,32]{1,2,0:T(8,128)(2,1)} all-reduce(bf16[3,224,32]{1,2,0:T(8,128)(2,1)} %pad_maximum_fusion.4), channel_id=1, replica_groups=mesh['node'=8,'grp'=4] {'grp'}, use_global_device_ids=true, to_apply=%region_0.0 | all-reduce | flops 21504 | bytes 86016 | tf_op jit(solution)/shard_map/psum | solution.py:65
  308.8 24.0 %psum.22 = f32[3,32,32]{1,2,0:T(8,128)} all-reduce(f32[3,32,32]{1,2,0:T(8,128)} %fusion.33), channel_id=1, replica_groups=mesh['node'=8,'grp'=4] {'node'}, use_global_device_ids=true, to_apply=%region_1.0 | all-reduce | flops 3072 | bytes 24576 | tf_op jit(solution)/shard_map/psum | solution.py:67
  339.2 3.6 cholesky.59
  344.8 3.8 custom-call.7
  348.5 3.6 cholesky.70
  354.1 3.2 custom-call.8
  360.5 3.6 cholesky.81
  366.0 3.2 custom-call.9
  373.8 5.7 %fusion = bf16[384,1792]{1,0:T(8,128)(2,1)} fusion(f32[384,1792]{1,0:T(8,128)} %fusion.46, bf16[384,1024]{1,0:T(8,128)(2,1)S(1)} %get-tuple-element.8, bf16[1792,1024]{1,0:T(8,128)(2,1)} %all-gather.8.cloned.1.call-done), kind=kOutput, calls=%fused_computation.1 | convolution fusion | flops 1410662400 | bytes 8585216 | tf_op jit(solution)/shard_map/dot_general | solution.py:47
  380.2 119.2 %all-reduce.2.cloned.1.call-done = f32[3,1024,32]{1,2,0:T(8,128)} async-done(((f32[3,1024,32]{1,2,0:T(8,128)}), f32[3,1024,32]{1,2,0:T(8,128)}) %all-reduce.2.cloned.1.call-update) | async-done | bytes 393232 | tf_op jit(solution)/shard_map/psum | solution.py:73
  (86 shorter events, 45.6 us)
Async XLA Ops:
  7.2 39.8 %all-gather.6.cloned.1.call-start = ((), (), s32[]{:S(2)}) async-start(), calls=%async_computation.2 | async-start | bytes 4128768 | tf_op jit(solution)/shard_map/all_gather | solution.py:34
  7.9 75.4 %all-gather.10.cloned.1.call-start = ((), (), s32[]{:S(2)}) async-start(), calls=%async_computation.4 | async-start | bytes 4128768 | tf_op jit(solution)/shard_map/all_gather | solution.py:32
  8.6 111.0 %all-gather.8.cloned.1.call-start = ((), (), s32[]{:S(2)}) async-start(), calls=%async_computation.3 | async-start | bytes 4128768 | tf_op jit(solution)/shard_map/all_gather | solution.py:33
  9.4 73.9 %copy-start.2 = (bf16[384,1792]{1,0:T(8,128)(2,1)S(1)}, bf16[384,1792]{1,0:T(8,128)(2,1)}, u32[]{:S(2)}) copy-start(bf16[384,1792]{1,0:T(8,128)(2,1)} %param.10) | copy-start | bytes 4128772
  9.4 194.9 %all-gather.14.cloned.1.call-start = ((), (), s32[]{:S(2)}) async-start(), calls=%async_computation.6 | async-start | bytes 7077888 | tf_op jit(solution)/shard_map/all_gather | solution.py:57
  126.0 148.4 %all-gather.12.cloned.1.call-start = ((), (), s32[]{:S(2)}) async-start(), calls=%async_computation.5 | async-start | bytes 14155776 | tf_op jit(solution)/shard_map/all_gather | solution.py:56
  128.2 1.3 copy-start.1
  131.1 29.4 %all-to-all-start.1 = ((bf16[384,8,224]{0,2,1:T(8,128)(2,1)}), bf16[384,8,224]{0,2,1:T(8,128)(2,1)S(1)}, u32[]{:S(2)}, u32[]{:S(2)}) async-start(bf16[384,8,224]{0,2,1:T(8,128)(2,1)} %bitcast.3), calls=%async_computation.1 | async-start | bytes 2752512 | tf_op jit(solution)/shard_map/all_to_all | solution.py:54
  160.5 37.1 %all-to-all-start = ((bf16[384,8,224]{0,2,1:T(8,128)(2,1)}), bf16[384,8,224]{0,2,1:T(8,128)(2,1)S(1)}, u32[]{:S(2)}, u32[]{:S(2)}) async-start(bf16[384,8,224]{0,2,1:T(8,128)(2,1)} %bitcast), calls=%async_computation | async-start | bytes 2752512 | tf_op jit(solution)/shard_map/all_to_all | solution.py:53
  164.1 335.3 %all-reduce.2.cloned.1.call-start = ((), (), s32[]{:S(2)}) async-start(), calls=%async_computation.7 | async-start | bytes 786432 | tf_op jit(solution)/shard_map/psum | solution.py:73
  197.6 1.3 copy-start.8
  198.9 5.4 %copy-start.4 = (bf16[8,28,8,384]{3,2,0,1:T(8,128)(2,1)S(1)}, bf16[8,28,8,384]{3,2,0,1:T(8,128)(2,1)}, u32[]{:S(2)}) copy-start(bf16[8,28,8,384]{3,2,0,1:T(8,128)(2,1)} %copy.25) | copy-start | bytes 4128772
  204.3 70.1 %copy-start.5 = (bf16[8,28,8,384]{3,2,0,1:T(8,128)(2,1)S(1)}, bf16[8,28,8,384]{3,2,0,1:T(8,128)(2,1)}, u32[]{:S(2)}) copy-start(bf16[8,28,8,384]{3,2,0,1:T(8,128)(2,1)} %copy.24) | copy-start | bytes 4128772
  274.4 6.4 %copy-start.3 = (bf16[1,224,3072]{2,1,0:T(8,128)(2,1)S(1)}, bf16[1,224,3072]{2,1,0:T(8,128)(2,1)}, u32[]{:S(2)}) copy-start(bf16[1,224,3072]{2,1,0:T(8,128)(2,1)} %param.15) | copy-start | bytes 4128772
  274.4 6.4 %copy-start.6 = (f32[224,1024]{1,0:T(8,128)S(1)}, f32[224,1024]{1,0:T(8,128)}, u32[]{:S(2)}) copy-start(f32[224,1024]{1,0:T(8,128)} %convolution_bitcast_fusion.1) | copy-start | bytes 2752516
  280.8 1.0 copy-start.16
  369.2 3.1 copy-start.9
  370.2 2.8 copy-start.14
  373.8 5.7 %copy-start.10 = (f32[32,224]{1,0:T(8,128)S(1)}, f32[32,224]{1,0:T(8,128)}, u32[]{:S(2)}) copy-start(f32[32,224]{1,0:T(8,128)} %fusion.32) | copy-start | bytes 86020
  373.8 5.7 %copy-start.12 = (f32[32,224]{1,0:T(8,128)S(1)}, f32[32,224]{1,0:T(8,128)}, u32[]{:S(2)}) copy-start(f32[32,224]{1,0:T(8,128)} %fusion.31) | copy-start | bytes 86020
  373.8 5.7 %copy-start.15 = (f32[32,224]{1,0:T(8,128)S(1)}, f32[32,224]{1,0:T(8,128)}, u32[]{:S(2)}) copy-start(f32[32,224]{1,0:T(8,128)} %copy-done.14) | copy-start | bytes 86020
  379.5 122.7 %copy-start.13 = (f32[32,224]{1,0:T(8,128)S(1)}, f32[32,224]{1,0:T(8,128)}, u32[]{:S(2)}) copy-start(f32[32,224]{1,0:T(8,128)} %fusion.31) | copy-start | bytes 86020
  500.4 3.7 copy-start
  500.4 2.7 copy-start.11
  (1 other events, 0.9 us)
Sparse Core Ops, SparseCore 0:
  9.9 37.0 all-gather.5
  48.9 34.3 all-gather.9
  85.2 34.3 all-gather.7
  126.1 74.4 all-gather.13
  202.4 71.9 all-gather.11
  373.9 125.4 all-reduce.1
where the time goes:
time: 514 us; the launch traced here: 512 us
  waiting for transfers between devices  342 us (67%)
  matrix products  54.2 us (11%)
  blocking collectives  44.5 us (9%)
  other arithmetic  35.7 us (7%)
  between operations  14.4 us (3%)
  local copies, waits for them, and re-layouts  13.4 us (3%)
  starting transfers between devices  7.6 us (1%)
    psum x1, waiting for transfers between devices, on_device(): q_new = lax.psum(col_terms, ('node', 'grp')) / group_count  119 us
    all_gather x1, waiting for transfers between devices, on_device(): piece_gu = lax.all_gather(gate_up, 'node', axis=0, tiled=True)  64.7 us
    all_gather x1, waiting for transfers between devices, on_device(): lax.all_gather(down_weight_t, 'node', axis=0, tiled=True)  37.6 us
    all_to_all x1, waiting for transfers between devices, on_device(): lax.all_to_all(tokens, 'node', split_axis=1, concat_axis=0, tiled=True)  31.9 us
    all_gather x1, waiting for transfers between devices, on_device(): lax.all_gather(up_weight, 'node', axis=0, tiled=True)  31.5 us
    all_gather x1, waiting for transfers between devices, on_device(): lax.all_gather(gate_weight, 'node', axis=0, tiled=True)  31.1 us
    all_to_all x1, waiting for transfers between devices, on_device(): lax.all_to_all(cotangent, 'node', split_axis=1, concat_axis=0, tiled=True)  24.3 us
    psum x1, blocking collectives, on_device(): gram_matrix = lax.psum(local_gram, 'node')  24 us
  transfers between devices with their start and end apart: 8, of which 7 were waited for; matrix products, arithmetic and copies ran while one was open for 7% of the time, Pallas kernels for 0%

commit v1 on v0

v1 whole, which is shorter than its diff:
```python
import functools
import math

import jax
import jax.numpy as jnp
from jax import lax
from jax.experimental import pallas as pl
from jax.experimental.pallas import tpu as pltpu
from jax.sharding import PartitionSpec as P

MESH = pl.DeviceIdType.MESH
F32, BF16 = jnp.float32, jnp.bfloat16
HIGHEST = lax.Precision.HIGHEST
LANES = 128


def gelu_parts(value):
    coeff = math.sqrt(2.0 / math.pi)
    square = value * value
    tanh_value = jnp.tanh(coeff * (value + 0.044715 * square * value))
    activation = 0.5 * value * (1.0 + tanh_value)
    slope = 0.5 * (1.0 + tanh_value) + 0.5 * value * (1.0 - tanh_value * tanh_value) * coeff * (
        1.0 + 3.0 * 0.044715 * square
    )
    return activation, slope


def dot(a, b, precision=None):
    return jnp.dot(a, b, preferred_element_type=F32, precision=precision)


def dot_nt(a, b, precision=None):
    return lax.dot_general(
        a, b, (((1,), (1,)), ((), ())), preferred_element_type=F32, precision=precision
    )


def subsets(items):
    found = [()]
    for item in items:
        found += [s + (item,) for s in found]
    return found


def kernel(
    n, g, rank, n_recv,
    tok, cot, w_gate, w_up, w_down, err, q_pad,
    tok_grad, new_err, p_out, q_out,
    full, tok_t, cot_t, act, ups, hid, d_up, d_gate, grads, *rest
):
    recv_bufs = rest[:n_recv]
    (merged, power, hat, block_diag, q_t, pw_all, gram_all, q_part, q_rs, q_grp, q_all,
     send_sems, recv_sems, local_sems) = rest[n_recv:]
    me, grp = lax.axis_index("node"), lax.axis_index("grp")
    rows, hidden = w_gate.shape
    depth = tok.shape[1]
    half = hidden // 2
    bits = n.bit_length() - 1
    tile = 256
    used = 3 * rank
    weights = (w_gate, w_up, w_down)

    barrier = pltpu.get_barrier_semaphore()
    for d in range(1, n):
        pl.semaphore_signal(barrier, inc=1, device_id=(lax.rem(me + d, n), grp), device_id_type=MESH)
    for d in range(1, g):
        pl.semaphore_signal(barrier, inc=1, device_id=(me, lax.rem(grp + d, g)), device_id_type=MESH)

    flip = [(1 << b) * (1 - 2 * lax.rem(me // (1 << b), 2)) for b in range(bits)]
    offset = lambda mask: sum((flip[b] for b in mask), 0)
    outer = list(range(1, bits))
    orders = [outer + [0], outer[::-1] + [0]]
    rs_orders = [[0] + outer, [0] + outer[::-1]]
    cols = [pl.ds(h * half, half) for h in range(2)]
    block = lambda index: pl.ds(pl.multiple_of(index * rows, rows), rows)

    count = [0]
    started = []

    def send(src, dst, node, group):
        copy = pltpu.make_async_remote_copy(
            src_ref=src, dst_ref=dst,
            send_sem=send_sems.at[count[0]], recv_sem=recv_sems.at[count[0]],
            device_id=(node, group), device_id_type=MESH,
        )
        count[0] += 1
        started.append(copy)
        copy.start()
        return copy

    locals_ = []
    for w in range(3):
        copy = pltpu.make_async_copy(weights[w], full.at[w, block(me)], local_sems.at[w])
        copy.start()
        locals_.append(copy)
    pl.semaphore_wait(barrier, n - 1 + g - 1)

    gathers = {}

    def gather_start(w, t):
        for h in range(2):
            bit = orders[h][t]
            gathers[w, t, h] = []
            for mask in subsets(orders[h][:t]):
                at = (w, block(me + offset(mask)), cols[h])
                src = weights[w].at[:, cols[h]] if t == 0 else full.at[at]
                gathers[w, t, h].append(send(src, full.at[at], me + flip[bit], grp))

    def gather_finish(w, t):
        for h in range(2):
            for copy in gathers[w, t, h]:
                copy.wait_recv()

    for w in range(3):
        gather_start(w, 0)

    @pl.loop(0, depth // tile)
    def _(i):
        at = pl.ds(pl.multiple_of(i * tile, tile), tile)
        tok_t[at, :] = tok[:, at].T
        cot_t[at, :] = cot[:, at].T

    merged[...] = jnp.zeros_like(merged)
    power[...] = jnp.zeros_like(power)
    hat[...] = jnp.zeros_like(hat)
    block_diag[...] = jnp.zeros_like(block_diag)
    q_t[...] = jnp.zeros_like(q_t)
    for copy in locals_:
        copy.wait()

    for t in range(1, bits - 1):
        for w in range(3):
            gather_finish(w, t - 1)
            gather_start(w, t)
    for w in range(2):
        gather_finish(w, bits - 2)
        gather_start(w, bits - 1)

    gather_finish(0, bits - 1)

    @pl.loop(0, hidden // tile)
    def _(j):
        at = pl.ds(pl.multiple_of(j * tile, tile), tile)
        act[:, at] = dot(tok[...], full[0, :, at])

    gather_finish(1, bits - 1)

    @pl.loop(0, hidden // tile)
    def _(j):
        at = pl.ds(pl.multiple_of(j * tile, tile), tile)
        up_pre = dot(tok[...], full[1, :, at])
        activation, slope = gelu_parts(act[:, at])
        act[:, at] = activation
        ups[:, at] = up_pre * slope
        hid[:, at] = (activation * up_pre).astype(BF16)

    reduces = {}

    def partial_grad(m, left, right):
        @pl.loop(0, depth // tile)
        def _(i):
            at = pl.ds(pl.multiple_of(i * tile, tile), tile)
            grads[m, at, :] = dot(left[at, :], right[...]).astype(BF16)

    def reduce_start(m, t):
        for h in range(2):
            bit = rs_orders[h][t]
            reduces[m, t, h] = []
            for slot, mask in enumerate(subsets(rs_orders[h][t + 1:])):
                src = grads.at[m, block(me + flip[bit] + offset(mask)), cols[h]]
                dst = recv_bufs[t].at[m, slot, :, cols[h]]
                reduces[m, t, h].append(send(src, dst, me + flip[bit], grp))

    def reduce_add(m, t):
        for h in range(2):
            for slot, mask in enumerate(subsets(rs_orders[h][t + 1:])):
                reduces[m, t, h][slot].wait_recv()
                at = block(me + offset(mask))
                total = (
                    grads[m, at, cols[h]].astype(F32) + recv_bufs[t][m, slot, :, cols[h]].astype(F32)
                )
                if t < bits - 1:
                    grads[m, at, cols[h]] = total.astype(BF16)
                else:
                    scale = 1.0 / math.sqrt(tok.shape[0] * n)
                    memory = err[0, :, pl.ds(m * hidden + h * half, half)].astype(F32)
                    merged[m, 0:rows, cols[h]] = total * scale + memory

    def advance(m, t):
        reduce_add(m, t - 1)
        reduce_start(m, t)

    partial_grad(2, cot_t, hid)
    reduce_start(2, 0)
    gather_finish(2, bits - 2)
    gather_start(2, bits - 1)
    gather_finish(2, bits - 1)

    @pl.loop(0, hidden // tile)
    def _(j):
        at = pl.ds(pl.multiple_of(j * tile, tile), tile)
        back = dot(cot[...], full[2, :, at])
        d_up[:, at] = (back * act[:, at]).astype(BF16)
        d_gate[:, at] = (back * ups[:, at]).astype(BF16)

    advance(2, 1)
    partial_grad(0, tok_t, d_gate)
    reduce_start(0, 0)
    partial_grad(1, tok_t, d_up)
    reduce_start(1, 0)
    advance(0, 1)

    def token_part(first, last):
        @pl.loop(first, last)
        def _(i):
            at = pl.ds(pl.multiple_of(i * tile, tile), tile)
            tok_grad[:, at] = (
                dot_nt(d_gate[...], full[0, at, :]) + dot_nt(d_up[...], full[1, at, :])
            ).astype(BF16)

    steps = depth // tile
    token_part(0, steps // 2)
    advance(1, 1)
    advance(2, 2)
    token_part(steps // 2, steps)
    advance(0, 2)
    advance(1, 2)
    for t in range(3, bits):
        for m in (2, 0, 1):
            advance(m, t)
    total = jnp.zeros((rows, LANES), F32)
    for m in (2, 0, 1):
        reduce_add(m, bits - 1)
        total += dot(merged[m, 0:rows, :], q_pad[m], HIGHEST)

    pw_all[grp] = total.astype(BF16)
    copies = [
        send(pw_all.at[grp], pw_all.at[grp], me, lax.rem(grp + d, g)) for d in range(1, g)
    ]
    for copy in copies:
        copy.wait_recv()
    total = pw_all[0].astype(F32)
    for k in range(1, g):
        total += pw_all[k].astype(F32)
    power[0:rows, :] = total * (1.0 / g)

    lane = lax.broadcasted_iota(jnp.int32, (rank, LANES), 1)
    row = lax.broadcasted_iota(jnp.int32, (rank, LANES), 0)
    padded = power[...]
    gram = dot(padded.T, padded, HIGHEST)
    picked = gram[0:rank]
    for m in range(1, 3):
        picked = jnp.where(lane >= m * rank, gram[m * rank:(m + 1) * rank], picked)
    gram_all[me] = picked
    copies = [
        send(gram_all.at[me], gram_all.at[me], lax.rem(me + d, n), grp) for d in range(1, n)
    ]
    for copy in copies:
        copy.wait_recv()
    picked = gram_all[0]
    for k in range(1, n):
        picked += gram_all[k]

    work = []
    for m in range(3):
        rolled = picked if m == 0 else pltpu.roll(picked, LANES - m * rank, 1)
        unit = jnp.where(lane == row + rank, 1.0, 0.0).astype(F32)
        work.append(jnp.where(lane < rank, rolled, unit))
    for j in range(rank):
        for m in range(3):
            a = work[m]
            inverse = 1.0 / jnp.sqrt(a[j:j + 1, j:j + 1])
            pivot_row = a[j:j + 1, :] * inverse
            column = a[:, j:j + 1] * inverse
            work[m] = jnp.where(row > j, a - column * pivot_row, jnp.where(row == j, pivot_row, a))
    for m in range(3):
        shift = ((m - 1) * rank) % LANES
        moved = work[m] if shift == 0 else pltpu.roll(work[m], shift, 1)
        inside = (lane >= m * rank) & (lane < (m + 1) * rank)
        block_diag[m * rank:(m + 1) * rank, :] = jnp.where(inside, moved, 0.0)
    hat[0:rows, :] = dot_nt(power[0:rows, :], block_diag[...], HIGHEST)
    p_out[...] = hat[0:rows, :]

    hat_t = hat[...].T
    c_blocks = min(n, hidden // LANES)
    r_blocks = n // c_blocks
    c_size, r_size = hidden // c_blocks, used // r_blocks
    for m in range(3):
        q_t[m * rank:(m + 1) * rank, :] = dot(hat_t[m * rank:(m + 1) * rank], merged[m], HIGHEST)
    spots = [
        (slice(c // c_blocks * r_size, (c // c_blocks + 1) * r_size),
         slice(c % c_blocks * c_size, (c % c_blocks + 1) * c_size))
        for c in range(n)
    ]
    for c in range(n):
        q_part[c] = q_t[spots[c]].astype(BF16)
    q_rs[me] = q_part[me]
    copies = []
    for d in range(1, n):
        to = lax.rem(me + d, n)
        copies.append(send(q_part.at[to], q_rs.at[me], to, grp))
    for copy in copies:
        copy.wait_recv()
    total = q_rs[0].astype(F32)
    for k in range(1, n):
        total += q_rs[k].astype(F32)
    q_grp[grp] = total.astype(BF16)
    copies = [send(q_grp.at[grp], q_grp.at[grp], me, lax.rem(grp + d, g)) for d in range(1, g)]
    for copy in copies:
        copy.wait_recv()
    total = q_grp[0].astype(F32)
    for k in range(1, g):
        total += q_grp[k].astype(F32)
    q_all[me] = (total * (1.0 / g)).astype(BF16)
    copies = [send(q_all.at[me], q_all.at[me], lax.rem(me + d, n), grp) for d in range(1, n)]
    for copy in copies:
        copy.wait_recv()
    for c in range(n):
        q_t[spots[c]] = q_all[c].astype(F32)
    q_out[...] = q_t[0:used, :]

    wide = lax.broadcasted_iota(jnp.int32, (rows, LANES), 1)
    for m in range(3):
        own = jnp.where((wide >= m * rank) & (wide < (m + 1) * rank), hat[0:rows, :], 0.0)
        for h in range(2):
            rebuilt = dot(own, q_t[:, cols[h]], HIGHEST)
            new_err[0, :, pl.ds(m * hidden + h * half, half)] = (
                merged[m, 0:rows, cols[h]] - rebuilt
            ).astype(BF16)
    for copy in started:
        copy.wait_send()


def on_device(n, g, tokens, cotangent, gate_weight, up_weight, down_weight_t, error_memory, q_init):
    token_rows, depth = tokens.shape
    rows, hidden = gate_weight.shape
    rank = q_init.shape[2]
    used = 3 * rank
    bits = n.bit_length() - 1
    padded = -(-rows // LANES) * LANES
    q_pad = jnp.stack(
        [jnp.pad(q_init[m], ((0, 0), (m * rank, LANES - (m + 1) * rank))) for m in range(3)]
    )
    c_blocks = min(n, hidden // LANES)
    chunk = (used // (n // c_blocks), hidden // c_blocks)
    copies = 12 * (n - 1) + 3 * (n - 1) + 2 * (g - 1)
    recv_shapes = [
        pltpu.VMEM((3, 1 << (bits - 1 - t), rows, hidden), BF16) for t in range(bits)
    ]
    vmem = pl.BlockSpec(memory_space=pltpu.VMEM)
    token_grad, new_error, hats, q_t = pl.pallas_call(
        functools.partial(kernel, n, g, rank, bits),
        out_shape=(
            jax.ShapeDtypeStruct((token_rows, depth), BF16),
            jax.ShapeDtypeStruct((1, rows, 3 * hidden), BF16),
            jax.ShapeDtypeStruct((rows, LANES), F32),
            jax.ShapeDtypeStruct((used, hidden), F32),
        ),
        in_specs=[vmem] * 7,
        out_specs=(vmem,) * 4,
        scratch_shapes=[
            pltpu.VMEM((3, depth, hidden), BF16),
            pltpu.VMEM((depth, token_rows), BF16),
            pltpu.VMEM((depth, token_rows), BF16),
            pltpu.VMEM((token_rows, hidden), F32),
            pltpu.VMEM((token_rows, hidden), F32),
            pltpu.VMEM((token_rows, hidden), BF16),
            pltpu.VMEM((token_rows, hidden), BF16),
            pltpu.VMEM((token_rows, hidden), BF16),
            pltpu.VMEM((3, depth, hidden), BF16),
            *recv_shapes,
            pltpu.VMEM((3, padded, hidden), F32),
            pltpu.VMEM((padded, LANES), F32),
            pltpu.VMEM((padded, LANES), F32),
            pltpu.VMEM((LANES, LANES), F32),
            pltpu.VMEM((LANES, hidden), F32),
            pltpu.VMEM((g, rows, LANES), BF16),
            pltpu.VMEM((n, rank, LANES), F32),
            pltpu.VMEM((n,) + chunk, BF16),
            pltpu.VMEM((n,) + chunk, BF16),
            pltpu.VMEM((g,) + chunk, BF16),
            pltpu.VMEM((n,) + chunk, BF16),
            pltpu.SemaphoreType.DMA((copies,)),
            pltpu.SemaphoreType.DMA((copies,)),
            pltpu.SemaphoreType.DMA((3,)),
        ],
        compiler_params=pltpu.CompilerParams(
            collective_id=0, has_side_effects=True, vmem_limit_bytes=67_043_328
        ),
    )(tokens, cotangent, gate_weight, up_weight, down_weight_t, error_memory, q_pad)
    p_hat = jnp.stack([hats[:, m * rank:(m + 1) * rank] for m in range(3)])
    q_new = q_t.reshape(3, rank, hidden).transpose(0, 2, 1)
    return token_grad, new_error, p_hat, q_new


def solution(mesh):
    return jax.shard_map(
        functools.partial(on_device, mesh.shape["node"], mesh.shape["grp"]),
        mesh=mesh,
        in_specs=(
            P(("node", "grp"), None),
            P(("node", "grp"), None),
            P("node", None),
            P("node", None),
            P("node", None),
            P("grp", "node", None),
            P(),
        ),
        out_specs=(P(("node", "grp"), None), P("grp", "node", None), P(None, "node", None), P()),
        check_vma=False,
    )
```

time: 514 us -> 155 us (0.30)
  waiting for transfers between devices: 342 us -> 0 us
  Pallas kernels: 0 us -> 144 us
  matrix products: 54.2 us -> 0 us
  blocking collectives: 44.5 us -> 0 us
  other arithmetic: 35.7 us -> 1.93 us
  between operations: 14.4 us -> 0.69 us
  starting transfers between devices: 7.6 us -> 0 us
  local copies, waits for them, and re-layouts: 13.4 us -> 8 us
    all_gather x5 -> x0, waiting for transfers between devices: 165 us -> none  [the longest x1 64.7 us: on_device(): piece_gu = lax.all_gather(gate_up, 'node', axis=0, tiled=True)]
    pallas_call x0 -> x1, Pallas kernels: none -> 144 us  [on_device(): pl.pallas_call(functools.partial(kernel, n, g, rank, bits), out_shape=(ja...]
    psum x1 -> x0, waiting for transfers between devices: 119 us -> none  [on_device(): q_new = lax.psum(col_terms, ('node', 'grp')) / group_count]
    all_to_all x2 -> x0, waiting for transfers between devices: 56.2 us -> none  [the longest x1 31.9 us: on_device(): lax.all_to_all(tokens, 'node', split_axis=1, concat_axis=0, tiled=True)]
    dot_general x17 -> x0, matrix products: 50 us -> none  [the longest x2 11.8 us: contract_rows(): lax.dot_general(left_side, right_side, (((0,), (0,)), ((), ())), preferre...]
    psum x2 -> x0, blocking collectives: 44.5 us -> none  [the longest x1 24 us: on_device(): gram_matrix = lax.psum(local_gram, 'node')]
    another operation x18 -> x2, other arithmetic: 28.8 us -> 1.93 us  [the longest x1 1.26 us: on_device(): jnp.stack([jnp.pad(q_init[m], ((0, 0), (m * rank, LANES - (m + 1) * rank)...]
    all_to_all x2 -> x0, starting transfers between devices: 7.18 us -> none  [the longest x1 3.61 us: on_device(): lax.all_to_all(cotangent, 'node', split_axis=1, concat_axis=0, tiled=True)]
  transfers between devices with their start and end apart: 8 -> 0, of which waited for: 7 -> 0; matrix products, arithmetic and copies ran while one was open for 7% -> 0% of each run, Pallas kernels for 0% -> 0%
where the time goes in v1:
time: 155 us
  Pallas kernels  144 us (93%)
  local copies, waits for them, and re-layouts  8 us (5%)
  other arithmetic  1.93 us (1%)
    pallas_call x1, Pallas kernels, on_device(): pl.pallas_call(functools.partial(kernel, n, g, rank, bits), out_shape=(ja...  144 us
    unnamed x10, local copies, waits for them, and re-layouts  5.18 us

profile of v1, /device:TPU:0, one launch (start us, length us, event | category | flops | bytes accessed | tf_op | source)
XLA Modules:
  0.0 154.7 jit_solution(7485004274608628222)
XLA Ops:
  0.6 1.1 fusion
  1.7 0.2 copy.21
  1.9 0.2 copy.22
  2.1 0.2 copy.23
  2.3 0.3 pad_bitcast_fusion
  2.7 1.3 pad_maximum_fusion.q_pad
  4.0 144.0 %shard_map.102 = (bf16[384,1792]{1,0:T(8,128)(2,1)}, bf16[1,224,3072]{2,1,0:T(8,128)(2,1)}, f32[224,128]{1,0:T(8,128)}, f32[96,1024]{1,0:T(8,128)}) custom-call(bf16[384,1792]{1,0:T(8,128)(2,1)} %tok.1, bf16[384,1792]{1,0:T(8,128)(2,1)} %cot.1, bf16[224,1024]{1,0:T(8,128)(2,1)} %w_gate.1, bf16[224,1024]{1,0:T(8,128)(2,1)} %w_up.1, bf16[224,1024]{1,0:T(8,128)(2,1)} %w_down.1, ...), custom_call_target="tpu_custom_call" | custom-call | tf_op jit(solution)/shard_map/pallas_call | solution.py:351
  148.0 1.2 slice_bitcast_fusion.2
  149.2 0.1 copy.18
  149.2 0.1 copy.20
  149.3 0.1 copy.19
  149.4 0.7 pad_maximum_fusion.1
  150.1 0.0 copy-start
  150.1 2.6 %copy.27 = bf16[384,1792]{1,0:T(8,128)(2,1)} copy(bf16[384,1792]{1,0:T(8,128)(2,1)} %get-tuple-element.28) | data formatting | bytes 2752512
  152.7 0.0 copy-done
  152.7 0.0 copy-start.1
  152.7 1.1 copy.28
  153.8 0.2 copy-done.1
  153.9 0.7 copy.29
  (1 shorter events, 0.0 us)
Async XLA Ops:
  150.1 2.6 %copy-start = (bf16[1,224,3072]{2,1,0:T(8,128)(2,1)S(1)}, bf16[1,224,3072]{2,1,0:T(8,128)(2,1)}, u32[]{:S(2)}) copy-start(bf16[1,224,3072]{2,1,0:T(8,128)(2,1)} %get-tuple-element.29) | copy-start | bytes 4128772
  152.7 1.2 copy-start.1

commit v2 on v1

--- a/solution.py
+++ b/solution.py
@@ -97,21 +97,28 @@
 
     gathers = {}
 
+    def gather_send(w, t, h, mask):
+        at = (w, block(me + offset(mask)), cols[h])
+        src = full.at[at] if mask else weights[w].at[:, cols[h]]
+        copy = send(src, full.at[at], me + flip[orders[h][t]], grp)
+        gathers.setdefault((w, t, h), []).append(copy)
+
     def gather_start(w, t):
         for h in range(2):
-            bit = orders[h][t]
-            gathers[w, t, h] = []
-            for mask in subsets(orders[h][:t]):
-                at = (w, block(me + offset(mask)), cols[h])
-                src = weights[w].at[:, cols[h]] if t == 0 else full.at[at]
-                gathers[w, t, h].append(send(src, full.at[at], me + flip[bit], grp))
+            held = subsets(orders[h][:t])
+            if t < bits - 1:
+                for mask in held:
+                    gather_send(w, t, h, mask)
+            for mask in held:
+                if t == 0 or orders[h][t - 1] in mask:
+                    gather_send(w, bits - 1, h, mask)
 
     def gather_finish(w, t):
         for h in range(2):
             for copy in gathers[w, t, h]:
                 copy.wait_recv()
 
-    for w in range(3):
+    for w in range(2):
         gather_start(w, 0)
 
     @pl.loop(0, depth // tile)
@@ -129,13 +136,12 @@
         copy.wait()
 
     for t in range(1, bits - 1):
-        for w in range(3):
+        for w in range(2):
             gather_finish(w, t - 1)
             gather_start(w, t)
-    for w in range(2):
-        gather_finish(w, bits - 2)
-        gather_start(w, bits - 1)
-
+    gather_start(2, 0)
+    gather_finish(0, bits - 2)
+    gather_start(0, bits - 1)
     gather_finish(0, bits - 1)
 
     @pl.loop(0, hidden // tile)
@@ -143,21 +149,33 @@
         at = pl.ds(pl.multiple_of(j * tile, tile), tile)
         act[:, at] = dot(tok[...], full[0, :, at])
 
+    gather_finish(1, bits - 2)
+    gather_start(1, bits - 1)
     gather_finish(1, bits - 1)
 
-    @pl.loop(0, hidden // tile)
-    def _(j):
-        at = pl.ds(pl.multiple_of(j * tile, tile), tile)
-        up_pre = dot(tok[...], full[1, :, at])
-        activation, slope = gelu_parts(act[:, at])
-        act[:, at] = activation
-        ups[:, at] = up_pre * slope
-        hid[:, at] = (activation * up_pre).astype(BF16)
+    def up_part(first, last):
+        @pl.loop(first, last)
+        def _(j):
+            at = pl.ds(pl.multiple_of(j * tile, tile), tile)
+            up_pre = dot(tok[...], full[1, :, at])
+            activation, slope = gelu_parts(act[:, at])
+            act[:, at] = activation
+            ups[:, at] = up_pre * slope
+            hid[:, at] = (activation * up_pre).astype(BF16)
+
+    tiles = hidden // tile
+    up_part(0, tiles // 2)
+    for t in range(1, bits - 1):
+        gather_finish(2, t - 1)
+        gather_start(2, t)
+    up_part(tiles // 2, tiles)
 
     reduces = {}
 
-    def partial_grad(m, left, right):
-        @pl.loop(0, depth // tile)
+    steps = depth // tile
+
+    def partial_grad(m, left, right, first=0, last=steps):
+        @pl.loop(first, last)
         def _(i):
             at = pl.ds(pl.multiple_of(i * tile, tile), tile)
             grads[m, at, :] = dot(left[at, :], right[...]).astype(BF16)
@@ -194,6 +212,7 @@
     reduce_start(2, 0)
     gather_finish(2, bits - 2)
     gather_start(2, bits - 1)
+    advance(2, 1)
     gather_finish(2, bits - 1)
 
     @pl.loop(0, hidden // tile)
@@ -203,12 +222,13 @@
         d_up[:, at] = (back * act[:, at]).astype(BF16)
         d_gate[:, at] = (back * ups[:, at]).astype(BF16)
 
-    advance(2, 1)
     partial_grad(0, tok_t, d_gate)
     reduce_start(0, 0)
-    partial_grad(1, tok_t, d_up)
+    advance(2, 2)
+    partial_grad(1, tok_t, d_up, 0, steps // 2)
+    advance(0, 1)
+    partial_grad(1, tok_t, d_up, steps // 2, steps)
     reduce_start(1, 0)
-    advance(0, 1)
 
     def token_part(first, last):
         @pl.loop(first, last)
@@ -218,12 +238,11 @@
                 dot_nt(d_gate[...], full[0, at, :]) + dot_nt(d_up[...], full[1, at, :])
             ).astype(BF16)
 
-    steps = depth // tile
-    token_part(0, steps // 2)
+    token_part(0, steps // 3)
     advance(1, 1)
-    advance(2, 2)
-    token_part(steps // 2, steps)
+    token_part(steps // 3, 2 * steps // 3)
     advance(0, 2)
+    token_part(2 * steps // 3, steps)
     advance(1, 2)
     for t in range(3, bits):
         for m in (2, 0, 1):

time: 155 us -> 149 us (0.961)
  Pallas kernels: 144 us -> 138 us
    pallas_call x1, Pallas kernels: 144 us -> 138 us  [on_device(): pl.pallas_call(functools.partial(kernel, n, g, rank, bits), out_shape=(ja...]
where the time goes in v2:
time: 149 us
  Pallas kernels  138 us (93%)
  local copies, waits for them, and re-layouts  8 us (5%)
  other arithmetic  1.93 us (1%)
    pallas_call x1, Pallas kernels, on_device(): pl.pallas_call(functools.partial(kernel, n, g, rank, bits), out_shape=(ja...  138 us
    unnamed x10, local copies, waits for them, and re-layouts  5.18 us

profile of v2, /device:TPU:0, one launch (start us, length us, event | category | flops | bytes accessed | tf_op | source)
XLA Modules:
  0.0 149.1 jit_solution(5493146110265331606)
XLA Ops:
  0.6 1.1 fusion
  1.7 0.2 copy.21
  1.9 0.2 copy.22
  2.1 0.2 copy.23
  2.3 0.3 pad_bitcast_fusion
  2.7 1.3 pad_maximum_fusion.q_pad
  4.0 138.4 %shard_map.102 = (bf16[384,1792]{1,0:T(8,128)(2,1)}, bf16[1,224,3072]{2,1,0:T(8,128)(2,1)}, f32[224,128]{1,0:T(8,128)}, f32[96,1024]{1,0:T(8,128)}) custom-call(bf16[384,1792]{1,0:T(8,128)(2,1)} %tok.1, bf16[384,1792]{1,0:T(8,128)(2,1)} %cot.1, bf16[224,1024]{1,0:T(8,128)(2,1)} %w_gate.1, bf16[224,1024]{1,0:T(8,128)(2,1)} %w_up.1, bf16[224,1024]{1,0:T(8,128)(2,1)} %w_down.1, ...), custom_call_target="tpu_custom_call" | custom-call | tf_op jit(solution)/shard_map/pallas_call | solution.py:370
  142.4 1.2 slice_bitcast_fusion.2
  143.6 0.1 copy.18
  143.7 0.1 copy.20
  143.7 0.1 copy.19
  143.8 0.7 pad_maximum_fusion.1
  144.5 0.0 copy-start
  144.5 2.6 %copy.27 = bf16[384,1792]{1,0:T(8,128)(2,1)} copy(bf16[384,1792]{1,0:T(8,128)(2,1)} %get-tuple-element.28) | data formatting | bytes 2752512
  147.1 0.0 copy-done
  147.1 0.0 copy-start.1
  147.1 1.1 copy.28
  148.2 0.2 copy-done.1
  148.3 0.7 copy.29
  (1 shorter events, 0.0 us)
Async XLA Ops:
  144.5 2.6 %copy-start = (bf16[1,224,3072]{2,1,0:T(8,128)(2,1)S(1)}, bf16[1,224,3072]{2,1,0:T(8,128)(2,1)}, u32[]{:S(2)}) copy-start(bf16[1,224,3072]{2,1,0:T(8,128)(2,1)} %get-tuple-element.29) | copy-start | bytes 4128772
  147.1 1.2 copy-start.1
